TPU v7x, 256 devices: a whole 4x4x8 slice. The times are simulated.
256 devices in a mesh: blk: 8 (over y, core), rep: 8 (over z), sub: 4 (over x).
Axes of the slice: x: 4, y: 4, z: 8, core: 2. Of those that a mesh axis runs over, the one named last changes fastest.
Arguments:
- image_embed: bfloat16 [16384, 1152], P(('blk', 'rep', 'sub')), may hold values from -60 to 60
- text_embed: bfloat16 [16384, 1152], P(('blk', 'rep', 'sub')), may hold values from -60 to 60
- image_ids: int32 [16384], P(('blk', 'rep', 'sub')), may hold values from 0 to 8191
- text_ids: int32 [16384], P(('blk', 'rep', 'sub')), may hold values from 0 to 8191
Outputs:
- image_grad: float32 [16384, 1152], P(('blk', 'rep', 'sub'))
- text_grad: float32 [16384, 1152], P(('blk', 'rep', 'sub'))
All inputs are finite; a program needn't handle non-finite values.
Results may differ from a plain program's by a relative error of at most 0.008.
Values may be sent and summed in bfloat16 or wider, within the bound.
A program may use at most 64 MiB of HBM per device.

v0:
```python
import jax
import jax.numpy as jnp
from jax import lax
from jax.sharding import PartitionSpec as P

logit_scale = 30.0
logit_bias = -3.0


def laid_out(parts, dim):
    lengths = list(parts.shape[1:])
    lengths[dim] *= parts.shape[0]
    return jnp.moveaxis(parts, 0, dim).reshape(lengths)


def sent_to_all(shard, axis):
    copies = jnp.broadcast_to(shard, (lax.axis_size(axis), *shard.shape))
    return lax.all_to_all(copies, axis, split_axis=0, concat_axis=0, tiled=True)


def collect(shard, axis, dim):
    return laid_out(sent_to_all(shard, axis), dim)


def split_up(shard, dim, size):
    before, after = (shard.shape[:dim], shard.shape[dim + 1 :])
    return jnp.moveaxis(shard.reshape(*before, size, -1, *after), dim, 0)


def sum_at_owner(shard, axis, dim):
    size = lax.axis_size(axis)
    parts = lax.all_to_all(split_up(shard, dim, size), axis, 0, 0, tiled=True)
    return jnp.sum(parts.astype(jnp.float32), axis=0)


def unit_rows(embed):
    values = embed.astype(jnp.float32)
    inverse = lax.rsqrt(jnp.sum(values * values, axis=1, keepdims=True) + 1e-06)
    return (values * inverse, inverse)


def project(unit, inverse, grad):
    along = jnp.sum(unit * grad, axis=1, keepdims=True)
    return (grad - unit * along) * inverse


def pair_weights(images, image_keys, texts, text_keys):
    pair_logits = lax.dot_general(
        images, texts, (((1,), (1,)), ((), ())), preferred_element_type=jnp.float32
    )
    pair_logits = logit_scale * pair_logits + logit_bias
    label_sign = (image_keys[:, None] == text_keys[None, :]).astype(jnp.float32)
    return (logit_scale * (jax.nn.sigmoid(pair_logits) - label_sign)).astype(jnp.bfloat16)


def image_term(gradient_factor, texts):
    return jnp.dot(gradient_factor, texts, preferred_element_type=jnp.float32)


def text_term(gradient_factor, images):
    return lax.dot_general(
        gradient_factor, images, (((0,), (0,)), ((), ())), preferred_element_type=jnp.float32
    )


def body(image_embed, text_embed, image_ids, text_ids):
    img_unit, img_inverse = unit_rows(image_embed)
    txt_unit, txt_inverse = unit_rows(text_embed)
    img_half = img_unit.astype(jnp.bfloat16)
    text_subset = txt_unit.astype(jnp.bfloat16)
    images, image_keys = (collect(img_half, "rep", 0), collect(image_ids, "rep", 0))
    texts, text_keys = (
        lax.all_gather(text_subset, ("blk", "sub"), axis=0, tiled=True),
        lax.all_gather(text_ids, ("blk", "sub"), axis=0, tiled=True),
    )
    gradient_factor = pair_weights(images, image_keys, texts, text_keys)
    g_img = sum_at_owner(image_term(gradient_factor, texts).astype(jnp.bfloat16), "rep", 0)
    g_txt = sum_at_owner(text_term(gradient_factor, images).astype(jnp.bfloat16), ("blk", "sub"), 0)
    return (project(img_unit, img_inverse, g_img), project(txt_unit, txt_inverse, g_txt))


def solution(mesh):
    return jax.shard_map(
        body,
        mesh=mesh,
        in_specs=(
            P(("blk", "rep", "sub"), None),
            P(("blk", "rep", "sub"), None),
            P(("blk", "rep", "sub")),
            P(("blk", "rep", "sub")),
        ),
        out_specs=(P(("blk", "rep", "sub"), None), P(("blk", "rep", "sub"), None)),
        check_vma=False,
    )
```

profile of v0, /device:TPU:1, one launch (start us, length us, event | category | flops | bytes accessed | tf_op | source)
XLA Modules:
  0.0 188.0 jit_solution(16053967134164432722)
XLA Ops:
  7.2 0.0 copy-start.4
  7.2 0.0 copy-start.3
  7.2 0.0 all-gather.2.cloned.1.call-start
  7.2 1.0 fusion.13
  8.3 1.7 fusion.2
  10.0 0.0 all-gather.2.cloned.1.call-update
  10.0 1.3 broadcast_in_dim.5
  11.2 9.0 %all-to-all-start.1 = ((s32[8,1,64]{2,1,0:T(1,128)}), s32[8,1,64]{2,1,0:T(1,128)S(1)}, u32[]{:S(2)}, u32[]{:S(2)}) async-start(s32[8,1,64]{2,1,0:T(1,128)} %broadcast_in_dim.5), calls=%async_computation.1 | async-start | bytes 8192 | tf_op jit(solution)/shard_map/all_to_all | solution.py:18
  20.2 1.0 fusion.9
  21.3 1.0 fusion.5
  22.3 4.4 %all-to-all-done.1 = s32[8,1,64]{2,1,0:T(1,128)S(1)} async-done(((s32[8,1,64]{2,1,0:T(1,128)}), s32[8,1,64]{2,1,0:T(1,128)S(1)}, u32[]{:S(2)}, u32[]{:S(2)}) %all-to-all-start.1) | async-done | bytes 2080 | tf_op jit(solution)/shard_map/all_to_all | solution.py:18
  26.7 1.2 broadcast_in_dim.4
  27.9 3.6 %all-to-all-start = ((bf16[8,64,1152]{2,1,0:T(8,128)(2,1)}), bf16[8,64,1152]{2,1,0:T(8,128)(2,1)S(1)}, u32[]{:S(2)}, u32[]{:S(2)}) async-start(bf16[8,64,1152]{2,1,0:T(8,128)(2,1)} %broadcast_in_dim.4), calls=%async_computation | async-start | bytes 2359296 | tf_op jit(solution)/shard_map/all_to_all | solution.py:18
  31.5 0.0 copy-done.4
  31.5 0.6 dynamic-slice
  32.8 0.0 copy-done.3
  32.8 0.3 dynamic-update-slice
  33.0 18.4 %all-reduce = s32[2048]{0:T(1024)S(1)} all-reduce(s32[2048]{0:T(1024)S(1)} %dynamic-update-slice), channel_id=1, replica_groups=mesh['blk'=8,'rep'=8,'sub'=4] {'blk','sub'}, use_global_device_ids=true, to_apply=%add | all-reduce | flops 2048 | bytes 16384
  51.4 0.5 broadcast.36
  52.0 0.7 reduce.3
  52.6 0.1 eq.15
  52.7 10.7 %all-to-all-done = bf16[8,64,1152]{2,1,0:T(8,128)(2,1)S(1)} async-done(((bf16[8,64,1152]{2,1,0:T(8,128)(2,1)}), bf16[8,64,1152]{2,1,0:T(8,128)(2,1)S(1)}, u32[]{:S(2)}, u32[]{:S(2)}) %all-to-all-start) | async-done | bytes 1179680 | tf_op jit(solution)/shard_map/all_to_all | solution.py:18
  63.4 3.7 %all-gather.2.cloned.1.call-done = bf16[2048,1152]{1,0:T(8,128)(2,1)} async-done(((bf16[64,1152]{1,0:T(8,128)(2,1)}), bf16[2048,1152]{1,0:T(8,128)(2,1)}) %all-gather.2.cloned.1.call-update) | async-done | bytes 4718608 | tf_op jit(solution)/shard_map/all_gather | solution.py:73
  67.1 0.0 copy-start.2
  67.1 6.2 %multiply_convert_fusion = bf16[512,2048]{1,0:T(8,128)(2,1)S(1)} fusion(bf16[512,1152]{1,0:T(8,128)(2,1)S(1)} %bitcast.11, bf16[2048,1152]{1,0:T(8,128)(2,1)} %all-gather.2.cloned.1.call-done, s32[2048]{0:T(1024)S(1)} %all-reduce, s32[512]{0:T(512)S(1)} %eq.15), kind=kOutput, calls=%fused_computation.2 | convolution fusion | flops 2426404864 | bytes 8005632 | tf_op jit(solution)/shard_map/dot_general | solution.py:48
  73.3 0.0 copy-done.2
  73.3 0.0 copy-start.5
  73.3 3.9 %convolution_convert_fusion.1 = bf16[512,1152]{1,0:T(8,128)(2,1)} fusion(bf16[512,2048]{1,0:T(8,128)(2,1)S(1)} %multiply_convert_fusion, bf16[2048,1152]{1,0:T(8,128)(2,1)S(1)} %copy-done.2), kind=kOutput, calls=%fused_computation.3 | convolution fusion | flops 2416508928 | bytes 7995392 | tf_op jit(solution)/shard_map/dot_general | solution.py:57
  77.2 0.0 copy-done.5
  77.2 6.7 %all-to-all-start.2 = ((bf16[8,64,1152]{2,1,0:T(8,128)(2,1)}), bf16[8,64,1152]{2,1,0:T(8,128)(2,1)S(1)}, u32[]{:S(2)}, u32[]{:S(2)}) async-start(bf16[8,64,1152]{2,1,0:T(8,128)(2,1)} %bitcast.2), calls=%async_computation.2 | async-start | bytes 2359296 | tf_op jit(solution)/shard_map/all_to_all | solution.py:32
  83.9 6.6 %convolution_convert_fusion = bf16[2048,1152]{1,0:T(8,128)(2,1)} fusion(bf16[512,2048]{1,0:T(8,128)(2,1)} %copy-done.5, bf16[512,1152]{1,0:T(8,128)(2,1)S(1)} %bitcast.12), kind=kOutput, calls=%fused_computation.1 | convolution fusion | flops 2418278400 | bytes 7995392 | tf_op jit(solution)/shard_map/dot_general | solution.py:61
  90.6 25.4 %all-to-all-done.2 = bf16[8,64,1152]{2,1,0:T(8,128)(2,1)S(1)} async-done(((bf16[8,64,1152]{2,1,0:T(8,128)(2,1)}), bf16[8,64,1152]{2,1,0:T(8,128)(2,1)S(1)}, u32[]{:S(2)}, u32[]{:S(2)}) %all-to-all-start.2) | async-done | bytes 1179680 | tf_op jit(solution)/shard_map/all_to_all | solution.py:32
  116.0 0.0 copy-start
  116.0 5.6 %all-to-all-start.3 = ((bf16[32,64,1152]{2,1,0:T(8,128)(2,1)}), bf16[32,64,1152]{2,1,0:T(8,128)(2,1)}, u32[]{:S(2)}, u32[]{:S(2)}) async-start(bf16[32,64,1152]{2,1,0:T(8,128)(2,1)} %bitcast.10), calls=%async_computation.3 | async-start | bytes 9437184 | tf_op jit(solution)/shard_map/all_to_all | solution.py:32
  121.6 0.0 copy-start.1
  121.6 0.2 convert_reduce_fusion.1
  121.8 0.0 copy-done
  121.8 0.2 fusion.6
  122.0 0.8 fusion.8
  122.9 54.3 %all-to-all-done.3 = bf16[32,64,1152]{2,1,0:T(8,128)(2,1)} async-done(((bf16[32,64,1152]{2,1,0:T(8,128)(2,1)}), bf16[32,64,1152]{2,1,0:T(8,128)(2,1)}, u32[]{:S(2)}, u32[]{:S(2)}) %all-to-all-start.3) | async-done | bytes 4718624 | tf_op jit(solution)/shard_map/all_to_all | solution.py:32
  177.1 3.0 %convert_reduce_fusion = f32[64,1152]{1,0:T(8,128)S(1)} fusion(bf16[32,64,1152]{2,1,0:T(8,128)(2,1)} %all-to-all-done.3), kind=kLoop, calls=%fused_computation | loop fusion | flops 4644864 | bytes 5013504 | tf_op jit(solution)/shard_map/reduce_sum | solution.py:33
  180.1 0.0 copy-done.1
  180.1 0.2 fusion.10
  180.4 0.8 fusion.12
  (3 shorter events, 0.0 us)
Async XLA Ops:
  7.2 24.3 %copy-start.4 = (u32[256]{0:T(256)S(1)}, u32[256]{0:T(256)}, u32[]{:S(2)}) copy-start(u32[256]{0:T(256)} %constant.16) | copy-start | bytes 3076
  7.2 25.6 %copy-start.3 = (s32[64]{0:T(128)S(1)}, s32[64]{0:T(128)}, u32[]{:S(2)}) copy-start(s32[64]{0:T(128)} %param.7) | copy-start | bytes 772
  7.2 59.9 %all-gather.2.cloned.1.call-start = ((), (), s32[]{:S(2)}) async-start(), calls=%async_computation.4 | async-start | bytes 4866048 | tf_op jit(solution)/shard_map/all_gather | solution.py:73
  11.2 15.5 %all-to-all-start.1 = ((s32[8,1,64]{2,1,0:T(1,128)}), s32[8,1,64]{2,1,0:T(1,128)S(1)}, u32[]{:S(2)}, u32[]{:S(2)}) async-start(s32[8,1,64]{2,1,0:T(1,128)} %broadcast_in_dim.5), calls=%async_computation.1 | async-start | bytes 8192 | tf_op jit(solution)/shard_map/all_to_all | solution.py:18
  27.9 35.5 %all-to-all-start = ((bf16[8,64,1152]{2,1,0:T(8,128)(2,1)}), bf16[8,64,1152]{2,1,0:T(8,128)(2,1)S(1)}, u32[]{:S(2)}, u32[]{:S(2)}) async-start(bf16[8,64,1152]{2,1,0:T(8,128)(2,1)} %broadcast_in_dim.4), calls=%async_computation | async-start | bytes 2359296 | tf_op jit(solution)/shard_map/all_to_all | solution.py:18
  67.1 6.2 %copy-start.2 = (bf16[2048,1152]{1,0:T(8,128)(2,1)S(1)}, bf16[2048,1152]{1,0:T(8,128)(2,1)}, u32[]{:S(2)}) copy-start(bf16[2048,1152]{1,0:T(8,128)(2,1)} %all-gather.2.cloned.1.call-done) | copy-start | bytes 14155780
  73.3 3.9 %copy-start.5 = (bf16[512,2048]{1,0:T(8,128)(2,1)}, bf16[512,2048]{1,0:T(8,128)(2,1)S(1)}, u32[]{:S(2)}) copy-start(bf16[512,2048]{1,0:T(8,128)(2,1)S(1)} %multiply_convert_fusion) | copy-start | bytes 6291460
  77.2 38.8 %all-to-all-start.2 = ((bf16[8,64,1152]{2,1,0:T(8,128)(2,1)}), bf16[8,64,1152]{2,1,0:T(8,128)(2,1)S(1)}, u32[]{:S(2)}, u32[]{:S(2)}) async-start(bf16[8,64,1152]{2,1,0:T(8,128)(2,1)} %bitcast.2), calls=%async_computation.2 | async-start | bytes 2359296 | tf_op jit(solution)/shard_map/all_to_all | solution.py:32
  116.0 5.8 %copy-start = (bf16[64,1152]{1,0:T(8,128)(2,1)S(1)}, bf16[64,1152]{1,0:T(8,128)(2,1)}, u32[]{:S(2)}) copy-start(bf16[64,1152]{1,0:T(8,128)(2,1)} %param.4) | copy-start | bytes 442372
  116.0 61.1 %all-to-all-start.3 = ((bf16[32,64,1152]{2,1,0:T(8,128)(2,1)}), bf16[32,64,1152]{2,1,0:T(8,128)(2,1)}, u32[]{:S(2)}, u32[]{:S(2)}) async-start(bf16[32,64,1152]{2,1,0:T(8,128)(2,1)} %bitcast.10), calls=%async_computation.3 | async-start | bytes 9437184 | tf_op jit(solution)/shard_map/all_to_all | solution.py:32
  121.6 58.5 %copy-start.1 = (bf16[64,1152]{1,0:T(8,128)(2,1)S(1)}, bf16[64,1152]{1,0:T(8,128)(2,1)}, u32[]{:S(2)}) copy-start(bf16[64,1152]{1,0:T(8,128)(2,1)} %param.5) | copy-start | bytes 442372
Sparse Core Ops, SparseCore 0:
  11.1 55.9 all-gather.1
where the time goes:
time: 190 us; the launch traced here: 188 us
  waiting for transfers between devices  98.5 us (52%)
  starting transfers between devices  24.9 us (13%)
  blocking collectives  18.4 us (10%)
  matrix products  16.7 us (9%)
  between operations  14.8 us (8%)
  other arithmetic  10.7 us (6%)
  local copies, waits for them, and re-layouts  3.93 us (2%)
    all_to_all x2, waiting for transfers between devices, sum_at_owner(): parts = lax.all_to_all(split_up(shard, dim, size), axis, 0, 0, tiled=True)  79.7 us
    unnamed x1, blocking collectives  18.4 us
    all_to_all x2, waiting for transfers between devices, sent_to_all(): return lax.all_to_all(copies, axis, split_axis=0, concat_axis=0, tiled=True)  15.1 us
    all_to_all x2, starting transfers between devices, sent_to_all(): return lax.all_to_all(copies, axis, split_axis=0, concat_axis=0, tiled=True)  12.6 us
    all_to_all x2, starting transfers between devices, sum_at_owner(): parts = lax.all_to_all(split_up(shard, dim, size), axis, 0, 0, tiled=True)  12.3 us
    dot_general x1, matrix products, text_term(): lax.dot_general(gradient_factor, images, (((0,), (0,)), ((), ())), prefer...  6.65 us
    dot_general x1, matrix products, pair_weights(): lax.dot_general(images, texts, (((1,), (1,)), ((), ())), preferred_elemen...  6.18 us
    dot_general x1, matrix products, image_term(): return jnp.dot(gradient_factor, texts, preferred_element_type=jnp.float32)  3.9 us
  transfers between devices with their start and end apart: 5, of which 5 were waited for; matrix products, arithmetic and copies ran while one was open for 8% of the time, Pallas kernels for 0%

commit v1 on v0

v1 whole, which is shorter than its diff:
```python
import jax
import jax.numpy as jnp
from jax import lax
from jax.experimental import pallas as pl
from jax.experimental.pallas import tpu as pltpu
from jax.sharding import PartitionSpec as P

SCALE = 30.0
BIAS = -3.0
ROWS = 64
D = 1152
MESH = pl.DeviceIdType.MESH
F32 = jnp.float32
BF16 = jnp.bfloat16

Z_ORDER = (4, 3, -3, 2, -2, 1, -1, 0)
T_ORDER = (
    (2, 2), (1, 2), (2, 1), (-1, 2), (2, -1), (0, 2), (2, 0), (1, 1),
    (-1, 1), (1, -1), (-1, -1), (0, 1), (1, 0), (0, -1), (-1, 0), (0, 0),
)
RING4 = (0, 1, -1, 2)


def near4(d):
    return (d + 1) % 4 - 1


def near8(d):
    return (d + 3) % 8 - 3


def img_row(lane, dz):
    return Z_ORDER.index(near8(dz)) * 128 + lane * 64


def txt_row(dx, dy):
    return T_ORDER.index((near4(dx), near4(dy))) * 64


def tid_row(dx, dy):
    return RING4.index(near4(dy)) * 4 + RING4.index(near4(dx))


def iid_row(dz):
    return Z_ORDER.index(near8(dz)) * 2


class Plan:
    def __init__(self):
        self.msgs = {}
        self.origin = {}
        self.rows = {"sb": 0, "rb": 0}

    def add(self, name, way, src, dst, terms=None):
        self.msgs[name] = (len(self.msgs), way, src, dst, terms)
        buf, row, n = dst
        for r in range(row, row + n):
            assert (buf, r) not in self.origin
            self.origin[(buf, r)] = name

    def room(self, buf, n):
        row = self.rows[buf]
        self.rows[buf] += n
        return row

    def reduce(self, name, way, n, pieces):
        src, dst = self.room("sb", n), self.room("rb", n)
        self.add(name, way, ("sb", src, n), ("rb", dst, n), pieces)
        return dst


def make_plan():
    p = Plan()
    p.add("id", "c", ("iid", iid_row(0), 1), ("iid", iid_row(0) + 1, 1))
    for k in range(4):
        p.add(f"izp{k}", "z+", ("iid", iid_row(-k), 2), ("iid", iid_row(-k - 1), 2))
        if k < 3:
            p.add(f"izm{k}", "z-", ("iid", iid_row(k), 2), ("iid", iid_row(k + 1), 2))
    p.add("itxp0", "x+", ("tid", tid_row(0, 0), 1), ("tid", tid_row(-1, 0), 1))
    p.add("itxm0", "x-", ("tid", tid_row(0, 0), 1), ("tid", tid_row(1, 0), 1))
    p.add("itxp1", "x+", ("tid", tid_row(-1, 0), 1), ("tid", tid_row(2, 0), 1))
    p.add("ityp0", "y+", ("tid", tid_row(0, 0), 4), ("tid", tid_row(0, -1), 4))
    p.add("itym0", "y-", ("tid", tid_row(0, 0), 4), ("tid", tid_row(0, 1), 4))
    p.add("ityp1", "y+", ("tid", tid_row(0, -1), 4), ("tid", tid_row(0, 2), 4))
    for k in range(4):
        for h in (0, 1):
            if k < 3 or h == 0:
                p.add(f"zp{k}{h}", "z+", ("img", img_row(0, -k) + 32 * h, 32),
                      ("img", img_row(0, -k - 1) + 32 * h, 32))
            if k < 3 or h == 1:
                p.add(f"zm{k}{h}", "z-", ("img", img_row(0, k) + 32 * h, 32),
                      ("img", img_row(0, k + 1) + 32 * h, 32))
    for dz in Z_ORDER:
        p.add(f"d{dz}", "c", ("img", img_row(0, dz), 64), ("img", img_row(1, dz), 64))
    for half, one, two, at in (("a", "x", "y", lambda u, v: txt_row(u, v)), ("b", "y", "x", lambda u, v: txt_row(v, u))):
        o = 0 if half == "a" else 32
        p.add(f"{half}1p0", one + "+", ("txt", at(0, 0) + o, 32), ("txt", at(-1, 0) + o, 32))
        p.add(f"{half}1m0", one + "-", ("txt", at(0, 0) + o, 32), ("txt", at(1, 0) + o, 32))
        p.add(f"{half}1p1", one + "+", ("txt", at(-1, 0) + o, 16), ("txt", at(2, 0) + o, 16))
        p.add(f"{half}1m1", one + "-", ("txt", at(1, 0) + o + 16, 16), ("txt", at(2, 0) + o + 16, 16))
        for u in RING4:
            p.add(f"{half}2p0{u}", two + "+", ("txt", at(u, 0) + o, 32), ("txt", at(u, -1) + o, 32))
            p.add(f"{half}2m0{u}", two + "-", ("txt", at(u, 0) + o, 32), ("txt", at(u, 1) + o, 32))
            p.add(f"{half}2p1{u}", two + "+", ("txt", at(u, -1) + o, 16), ("txt", at(u, 2) + o, 16))
            p.add(f"{half}2m1{u}", two + "-", ("txt", at(u, 1) + o + 16, 16), ("txt", at(u, 2) + o + 16, 16))
    part = {}
    for dz in Z_ORDER:
        part[dz] = p.reduce(f"e{dz}", "c", 64, [(0, 64, [("gi", img_row(1, dz))])])
    got = {}
    for s, way in ((1, "z+"), (-1, "z-")):
        c = "p" if s == 1 else "m"
        for j in (4, 3, 2, 1):
            dz = near8(s * j)
            for h in ((0, 1) if s == 1 else (1, 0)):
                if j == 4 and h != (0 if s == 1 else 1):
                    continue
                terms = [("gi", img_row(0, dz) + 32 * h), ("rb", part[dz] + 32 * h)]
                if (s, j, h) in got:
                    terms.append(("rb", got[(s, j, h)]))
                got[(s, j - 1, h)] = p.reduce(f"rz{c}{j}{h}", way, 32, [(0, 32, terms)])
    p.final_img = [
        (32 * h, 32, [("gi", img_row(0, 0) + 32 * h), ("rb", part[0] + 32 * h),
                      ("rb", got[(1, 0, h)]), ("rb", got[(-1, 0, h)])])
        for h in (0, 1)
    ]
    p.final_txt = []
    for half, one, two, at in (("a", "x", "y", lambda u, v: txt_row(u, v)), ("b", "y", "x", lambda u, v: txt_row(v, u))):
        o = 0 if half == "a" else 32
        base = {}
        for u in RING4:
            far, last = {}, {}
            for s, c, q in ((1, "p", 0), (-1, "m", 16)):
                far[s] = p.reduce(f"r{half}2{c}2{u}", f"{two}{'+' if s == 1 else '-'}", 16,
                                  [(0, 16, [("gt", at(u, 2) + o + q)])])
            for s, c, q in ((1, "p", 0), (-1, "m", 16)):
                pieces = [(f, 16, [("gt", at(u, s) + o + f)] + ([("rb", far[s])] if f == q else [])) for f in (0, 16)]
                last[s] = p.reduce(f"r{half}2{c}1{u}", f"{two}{'+' if s == 1 else '-'}", 32, pieces)
            base[u] = [[("gt", at(u, 0) + o + f), ("rb", last[1] + f), ("rb", last[-1] + f)] for f in (0, 16)]
        far, last = {}, {}
        for s, c, q in ((1, "p", 0), (-1, "m", 16)):
            far[s] = p.reduce(f"r{half}1{c}2", f"{one}{'+' if s == 1 else '-'}", 16, [(0, 16, base[2][q // 16])])
        for s, c, q in ((1, "p", 0), (-1, "m", 16)):
            pieces = [(f, 16, base[s][f // 16] + ([("rb", far[s])] if f == q else [])) for f in (0, 16)]
            last[s] = p.reduce(f"r{half}1{c}1", f"{one}{'+' if s == 1 else '-'}", 32, pieces)
        p.final_txt += [(o + f, 16, base[0][f // 16] + [("rb", last[1] + f), ("rb", last[-1] + f)]) for f in (0, 16)]
    return p


PLAN = make_plan()


def both(stem, *tails):
    return [f"{stem}{c}{t}" for t in tails for c in "pm"]


def schedule():
    s = []
    send = lambda *names: s.append(("send", names))
    send("id", "itxp0", "itxm0")
    send("a1p0", "a1m0", "b1p0", "b1m0", "zp00", "zm01", "zp01", "zm00")
    send("a2p00", "a2m00", "b2p00", "b2m00", "d0")
    send("izp0", "izm0", "itxp1")
    send("zp10", "zm11")
    send("a1p1", "a1m1", "b1p1", "b1m1")
    for u in (-1, 1):
        send(*both("a2", f"0{u}"), *both("b2", f"0{u}"))
    send("ityp0", "itym0", "izp1", "izm1")
    send("zp11", "zm10", "d-1", "d1")
    send("ityp1", "izp2", "izm2", "izp3")
    send(*both("a2", "02"), *both("b2", "02"))
    send(*both("a2", "10"), *both("b2", "10"))
    send("zp20", "zm21")
    s.append(("tile", 3, 3))
    send(*both("a2", "1-1"), *both("b2", "1-1"))
    send("zp21", "zm20", "d-2", "d2")
    send(*both("a2", "11"), *both("b2", "11"))
    s.append(("tile", 3, 2))
    send("zp30", "zm31")
    s.append(("tile", 2, 3))
    send(*both("a2", "12"), *both("b2", "12"))
    s.append(("tile", 2, 2))
    send("d-3", "d3")
    s.append(("tile", 1, 3))
    s.append(("tile", 1, 2))
    s.append(("tile", 3, 1))
    s.append(("tile", 2, 1))
    send("d4")
    s.append(("tile", 1, 1))
    s.append(("tile", 3, 0))
    s.append(("tile", 2, 0))
    s.append(("tile", 1, 0))
    for t in (3, 2, 1, 0):
        s.append(("tile", 0, t))
    s.append(("gi", 0))
    send("e4", "e3")
    s.append(("gt", 0))
    for u in (2, 1):
        send(*both("ra2", f"2{u}"), *both("rb2", f"2{u}"))
    send(*both("ra2", "2-1"))
    send("rzp40", "rzm41", "rzp31")
    s.append(("gt", 1))
    send(*both("rb2", "2-1"), *both("ra2", "20"), *both("rb2", "20"))
    s.append(("gi", 1))
    send("e-3", "e2")
    send(*both("ra2", "12"), *both("rb2", "12"))
    send("rzm30", "rzp30", "rzm31")
    s.append(("gt", 2))
    send(*both("ra2", "11"), *both("rb2", "11"))
    s.append(("gi", 2))
    send("e-2", "e1")
    send("rzp21", "rzm20")
    s.append(("gt", 3))
    send(*both("ra2", "1-1"), *both("rb2", "1-1"))
    send("rzp20", "rzm21")
    s.append(("gi", 3))
    send("e-1", "e0")
    send("rzp11", "rzm10")
    send(*both("ra1", "2"), *both("rb1", "2"))
    send(*both("ra2", "10"), *both("rb2", "10"))
    send("rzp10", "rzm11")
    send(*both("ra1", "1"), *both("rb1", "1"))
    s.append(("out", "i"))
    s.append(("out", "t"))
    return s


def kernel(ie_ref, te_ref, ii_ref, ti_ref, oi_ref, ot_ref,
           img, txt, coef, gi, gt, sb, rb, iid, tid, icol, ssem, rsem):
    blk, rep, sub = lax.axis_index("blk"), lax.axis_index("rep"), lax.axis_index("sub")
    where = {
        "x+": {"sub": lax.rem(sub + 1, 4)}, "x-": {"sub": lax.rem(sub + 3, 4)},
        "y+": {"blk": lax.rem(blk + 2, 8)}, "y-": {"blk": lax.rem(blk + 6, 8)},
        "z+": {"rep": lax.rem(rep + 1, 8)}, "z-": {"rep": lax.rem(rep + 7, 8)},
        "c": {"blk": blk + 1 - 2 * lax.rem(blk, 2)},
    }
    barrier = pltpu.get_barrier_semaphore()
    for way in where.values():
        pl.semaphore_signal(barrier, inc=1, device_id=way, device_id_type=MESH)

    def unit(ref):
        v = ref[...].astype(F32)
        inv = lax.rsqrt(jnp.sum(v * v, axis=1, keepdims=True) + 1e-6)
        return v * inv, inv

    img[pl.ds(img_row(0, 0), ROWS), :] = unit(ie_ref)[0].astype(BF16)
    txt[pl.ds(txt_row(0, 0), ROWS), :] = unit(te_ref)[0].astype(BF16)
    for ids, ref, row in ((ii_ref, iid, iid_row(0)), (ti_ref, tid, tid_row(0, 0))):
        ref[row] = jnp.concatenate([ids[...], ids[...]], axis=1)
    pl.semaphore_wait(barrier, len(where))

    bufs = {"img": img, "txt": txt, "gi": gi, "gt": gt, "sb": sb, "rb": rb, "iid": iid, "tid": tid}

    def copy(name):
        index, way, src, dst, _ = PLAN.msgs[name]
        return pltpu.make_async_remote_copy(
            src_ref=bufs[src[0]].at[pl.ds(src[1], src[2])],
            dst_ref=bufs[dst[0]].at[pl.ds(dst[1], dst[2])],
            send_sem=ssem.at[index], recv_sem=rsem.at[index],
            device_id=where[way], device_id_type=MESH,
        )

    here, sent = set(), []

    def need(buf, row, n):
        for r in range(row, row + n):
            name = PLAN.origin.get((buf, r))
            if name is not None and name not in here:
                here.add(name)
                copy(name).wait_recv()

    def total(n, terms):
        acc = None
        for buf, row in terms:
            need(buf, row, n)
            v = bufs[buf][pl.ds(row, n), :].astype(F32)
            acc = v if acc is None else acc + v
        return acc

    def send(name):
        _, _, src, _, pieces = PLAN.msgs[name]
        if pieces is None:
            need(*src)
        else:
            for off, n, terms in pieces:
                sb[pl.ds(src[1] + off, n), :] = total(n, terms).astype(BF16)
        copy(name).start()
        sent.append(name)

    lane = lax.broadcasted_iota(jnp.int32, (1, 128), 1)
    ready = set()

    def columns(i):
        if i in ready:
            return
        ready.add(i)
        for p in (2 * i, 2 * i + 1):
            need("iid", 2 * p, 2)
            both_ids = jnp.where(lane < 64, iid[2 * p], iid[2 * p + 1])
            icol[pl.ds(128 * p, 128), :] = jnp.transpose(jnp.broadcast_to(both_ids, (128, 128)))

    def tile(i, t):
        need("img", 256 * i, 256)
        need("txt", 256 * t, 256)
        columns(i)
        keys = []
        for b in (4 * t, 4 * t + 2):
            r0, r1 = tid_row(*T_ORDER[b]), tid_row(*T_ORDER[b + 1])
            need("tid", r0, 1)
            need("tid", r1, 1)
            keys.append(jnp.where(lane < 64, tid[r0], tid[r1]))
        z = lax.dot_general(img[pl.ds(256 * i, 256), :], txt[pl.ds(256 * t, 256), :],
                            (((1,), (1,)), ((), ())), preferred_element_type=F32)
        sig = jax.nn.sigmoid(SCALE * z + BIAS)
        rows = icol[pl.ds(256 * i, 256), :]
        same = jnp.concatenate([(rows == k).astype(F32) for k in keys], axis=1)
        coef[pl.ds(256 * i, 256), pl.ds(256 * t, 256)] = (SCALE * (sig - same)).astype(BF16)

    def finish(pieces, ref, out):
        u, inv = unit(ref)
        for off, n, terms in pieces:
            g = total(n, terms)
            uu = u[off:off + n]
            along = jnp.sum(uu * g, axis=1, keepdims=True)
            out[pl.ds(off, n), :] = (g - uu * along) * inv[off:off + n]

    for step in schedule():
        if step[0] == "send":
            for name in step[1]:
                send(name)
        elif step[0] == "tile":
            tile(step[1], step[2])
        elif step[0] == "gi":
            rows = pl.ds(256 * step[1], 256)
            gi[rows, :] = jnp.dot(coef[rows, :], txt[...], preferred_element_type=F32)
        elif step[0] == "gt":
            rows = pl.ds(256 * step[1], 256)
            gt[rows, :] = lax.dot_general(coef[:, rows], img[...], (((0,), (0,)), ((), ())),
                                          preferred_element_type=F32)
        elif step[1] == "i":
            finish(PLAN.final_img, ie_ref, oi_ref)
        else:
            finish(PLAN.final_txt, te_ref, ot_ref)
    assert len(sent) == len(PLAN.msgs) and len(here) == len(PLAN.msgs)
    for name in sent:
        copy(name).wait_send()


def body(image_embed, text_embed, image_ids, text_ids):
    vmem = pl.BlockSpec(memory_space=pltpu.VMEM)
    n = len(PLAN.msgs)
    out = jax.ShapeDtypeStruct((ROWS, D), F32)
    return pl.pallas_call(
        kernel,
        name="pairs",
        out_shape=(out, out),
        in_specs=[vmem] * 4,
        out_specs=(vmem, vmem),
        scratch_shapes=[
            pltpu.VMEM((1024, D), BF16),
            pltpu.VMEM((1024, D), BF16),
            pltpu.VMEM((1024, 1024), BF16),
            pltpu.VMEM((1024, D), F32),
            pltpu.VMEM((1024, D), F32),
            pltpu.VMEM((PLAN.rows["sb"], D), BF16),
            pltpu.VMEM((PLAN.rows["rb"], D), BF16),
            pltpu.VMEM((16, 1, 128), jnp.int32),
            pltpu.VMEM((16, 1, 128), jnp.int32),
            pltpu.VMEM((1024, 128), jnp.int32),
            pltpu.SemaphoreType.DMA((n,)),
            pltpu.SemaphoreType.DMA((n,)),
        ],
        compiler_params=pltpu.CompilerParams(
            collective_id=0, has_side_effects=True, vmem_limit_bytes=60 * 1024 * 1024
        ),
    )(image_embed, text_embed, image_ids.reshape(1, ROWS), text_ids.reshape(1, ROWS))


def solution(mesh):
    rows = P(("blk", "rep", "sub"), None)
    flat = P(("blk", "rep", "sub"))
    return jax.shard_map(
        body, mesh=mesh, in_specs=(rows, rows, flat, flat), out_specs=(rows, rows), check_vma=False
    )
```

time: 190 us -> 58.9 us (0.31)
  waiting for transfers between devices: 98.5 us -> 0 us
  Pallas kernels: 0 us -> 55.3 us
  starting transfers between devices: 24.9 us -> 0 us
  blocking collectives: 18.4 us -> 0 us
  matrix products: 16.7 us -> 0 us
  between operations: 14.8 us -> 0.65 us
  other arithmetic: 10.7 us -> 0 us
    all_to_all x4 -> x0, waiting for transfers between devices: 94.8 us -> none  [the longest x2 79.7 us: sum_at_owner(): parts = lax.all_to_all(split_up(shard, dim, size), axis, 0, 0, tiled=True)]
    pallas_call x0 -> x1, Pallas kernels: none -> 55.3 us  [body(): pl.pallas_call(kernel, name='pairs', out_shape=(out, out), in_specs=[vmem...]
    all_to_all x4 -> x0, starting transfers between devices: 24.9 us -> none  [the longest x2 12.6 us: sent_to_all(): return lax.all_to_all(copies, axis, split_axis=0, concat_axis=0, tiled=True)]
    unnamed x1 -> x0, blocking collectives: 18.4 us -> none
    dot_general x3 -> x0, matrix products: 16.7 us -> none  [the longest x1 6.65 us: text_term(): lax.dot_general(gradient_factor, images, (((0,), (0,)), ((), ())), prefer...]
    reduce_sum x6 -> x0, other arithmetic: 5.66 us -> none  [the longest x2 3.17 us: sum_at_owner(): return jnp.sum(parts.astype(jnp.float32), axis=0)]
    all_gather x1 -> x0, waiting for transfers between devices: 3.7 us -> none  [body(): lax.all_gather(text_subset, ('blk', 'sub'), axis=0, tiled=True)]
    convert_element_type x2 -> x0, other arithmetic: 2.68 us -> none  [the longest x1 1.67 us: body(): text_subset = txt_unit.astype(jnp.bfloat16)]
  transfers between devices with their start and end apart: 5 -> 0, of which waited for: 5 -> 0; matrix products, arithmetic and copies ran while one was open for 8% -> 0% of each run, Pallas kernels for 0% -> 0%
where the time goes in v1:
time: 58.9 us; the launch traced here: 58.4 us
  Pallas kernels  55.3 us (94%)
  local copies, waits for them, and re-layouts  2.46 us (4%)
  between operations  0.65 us (1%)
    pallas_call x1, Pallas kernels, body(): pl.pallas_call(kernel, name='pairs', out_shape=(out, out), in_specs=[vmem...  55.3 us
    unnamed x4, local copies, waits for them, and re-layouts  2.46 us

profile of v1, /device:TPU:1, one launch (start us, length us, event | category | flops | bytes accessed | tf_op | source)
XLA Modules:
  0.0 58.4 jit_solution(10250215591141863236)
XLA Ops:
  0.6 55.3 %pairs.1 = (f32[64,1152]{1,0:T(8,128)}, f32[64,1152]{1,0:T(8,128)}) custom-call(bf16[64,1152]{1,0:T(8,128)(2,1)} %ie_ref.1, bf16[64,1152]{1,0:T(8,128)(2,1)} %te_ref.1, s32[1,64]{1,0:T(1,128)} %bitcast.2, s32[1,64]{1,0:T(1,128)} %bitcast.3), custom_call_target="tpu_custom_call" | custom-call | tf_op jit(solution)/shard_map/pairs/pallas_call | solution.py:352
  55.9 0.0 copy-start
  55.9 1.7 %copy.8 = f32[64,1152]{1,0:T(8,128)} copy(f32[64,1152]{1,0:T(8,128)} %get-tuple-element.4) | data formatting | bytes 589824
  57.6 0.0 copy-done
  57.6 0.7 %copy.9 = f32[64,1152]{1,0:T(8,128)} copy(f32[64,1152]{1,0:T(8,128)S(1)} %copy-done) | data formatting | bytes 589824
Async XLA Ops:
  55.9 1.8 %copy-start = (f32[64,1152]{1,0:T(8,128)S(1)}, f32[64,1152]{1,0:T(8,128)}, u32[]{:S(2)}) copy-start(f32[64,1152]{1,0:T(8,128)} %get-tuple-element.5) | copy-start | bytes 884740

commit v2 on v1

v2 whole, which is shorter than its diff:
```python
import jax
import jax.numpy as jnp
from jax import lax
from jax.experimental import pallas as pl
from jax.experimental.pallas import tpu as pltpu
from jax.sharding import PartitionSpec as P

SCALE = 30.0
BIAS = -3.0
ROWS = 64
D = 1152
UNIT = 16
GATHER_XY, REDUCE_XY = 32, 32
PARTS_Z = {1: ((0, 16), (16, 16), (32, 16), (48, 16)), -1: ((48, 16), (32, 16), (16, 16), (0, 16))}
IMG_CHUNKS = ((0, 256), (256, 256), (512, 256), (768, 256))
TXT_CHUNKS = ((0, 256), (256, 256), (512, 256), (768, 256))
MESH = pl.DeviceIdType.MESH
F32 = jnp.float32
BF16 = jnp.bfloat16

Z_ORDER = (4, 3, -3, 2, -2, 1, -1, 0)
T_ORDER = (
    (2, 2), (1, 2), (2, 1), (-1, 2), (2, -1), (0, 2), (2, 0), (1, 1),
    (-1, 1), (1, -1), (-1, -1), (0, 1), (1, 0), (0, -1), (-1, 0), (0, 0),
)
RING4 = (0, 1, -1, 2)


def near4(d):
    return (d + 1) % 4 - 1


def near8(d):
    return (d + 3) % 8 - 3


def img_row(lane, dz):
    return Z_ORDER.index(near8(dz)) * 128 + lane * 64


def txt_row(dx, dy):
    return T_ORDER.index((near4(dx), near4(dy))) * 64


def tid_row(dx, dy):
    return RING4.index(near4(dy)) * 4 + RING4.index(near4(dx))


def iid_row(dz):
    return Z_ORDER.index(near8(dz)) * 2


class Plan:
    def __init__(self):
        self.msgs = []
        self.origin = {}
        self.rows = {"sb": 0, "rb": 0}

    def add(self, way, src, dst, pieces=None):
        buf, row, n = dst
        for r in range(row, row + n):
            assert (buf, r) not in self.origin
            self.origin[buf, r] = len(self.msgs)
        self.msgs.append((way, src, dst, pieces))

    def room(self, buf, n):
        row = self.rows[buf]
        self.rows[buf] += n
        return row

    def reduce(self, way, n, *pieces):
        src, dst = self.room("sb", n), self.room("rb", n)
        self.add(way, ("sb", src, n), ("rb", dst, n), pieces)
        return dst


SIDES = ((1, "+"), (-1, "-"))
HALVES = ((0, "x", "y", lambda u, v: txt_row(u, v)), (32, "y", "x", lambda u, v: txt_row(v, u)))


def make_plan():
    p = Plan()
    p.add("c", ("iid", iid_row(0), 1), ("iid", iid_row(0) + 1, 1))
    for k in range(4):
        p.add("z+", ("iid", iid_row(-k), 2), ("iid", iid_row(-k - 1), 2))
        if k < 3:
            p.add("z-", ("iid", iid_row(k), 2), ("iid", iid_row(k + 1), 2))
    p.add("x+", ("tid", tid_row(0, 0), 1), ("tid", tid_row(-1, 0), 1))
    p.add("x-", ("tid", tid_row(0, 0), 1), ("tid", tid_row(1, 0), 1))
    p.add("x+", ("tid", tid_row(-1, 0), 1), ("tid", tid_row(2, 0), 1))
    p.add("y+", ("tid", tid_row(0, 0), 4), ("tid", tid_row(0, -1), 4))
    p.add("y-", ("tid", tid_row(0, 0), 4), ("tid", tid_row(0, 1), 4))
    p.add("y+", ("tid", tid_row(0, -1), 4), ("tid", tid_row(0, 2), 4))
    for k in range(4):
        for s, w in SIDES:
            for q, n in PARTS_Z[s]:
                if k < 3 or (q < 32) == (s == 1):
                    p.add("z" + w, ("img", img_row(0, -s * k) + q, n), ("img", img_row(0, -s * (k + 1)) + q, n))
    for dz in Z_ORDER:
        for h in (0, 1):
            p.add("c", ("img", img_row(0, dz) + 32 * h, 32), ("img", img_row(1, dz) + 32 * h, 32))
    for o, one, two, at in HALVES:
        n = GATHER_XY
        for s, w in SIDES:
            for q in range(0, 32, n):
                p.add(one + w, ("txt", at(0, 0) + o + q, n), ("txt", at(-s, 0) + o + q, n))
                for u in RING4:
                    p.add(two + w, ("txt", at(u, 0) + o + q, n), ("txt", at(u, -s) + o + q, n))
            e = o if s == 1 else o + UNIT
            p.add(one + w, ("txt", at(-s, 0) + e, UNIT), ("txt", at(2, 0) + e, UNIT))
            for u in RING4:
                p.add(two + w, ("txt", at(u, -s) + e, UNIT), ("txt", at(u, 2) + e, UNIT))
    part = {}
    for dz in Z_ORDER:
        for h in (0, 1):
            row = p.reduce("c", 32, [("gi", img_row(1, dz) + 32 * h)])
            part[dz, 2 * h], part[dz, 2 * h + 1] = row, row + UNIT
    got = {}
    for j in (4, 3, 2, 1):
        for s, w in SIDES:
            for q, n in PARTS_Z[s]:
                if j == 4 and (q < 32) != (s == 1):
                    continue
                dz, pieces = near8(s * j), []
                for e in range(q // UNIT, (q + n) // UNIT):
                    terms = [("gi", img_row(0, dz) + UNIT * e), ("rb", part[dz, e])]
                    if (s, j, e) in got:
                        terms.append(("rb", got[s, j, e]))
                    pieces.append(terms)
                row = p.reduce("z" + w, n, *pieces)
                for k in range(n // UNIT):
                    got[s, j - 1, q // UNIT + k] = row + UNIT * k
    p.final_img = [
        (UNIT * q, [("gi", img_row(0, 0) + UNIT * q), ("rb", part[0, q]), ("rb", got[1, 0, q]), ("rb", got[-1, 0, q])])
        for q in range(4)
    ]
    p.final_txt = []
    for o, one, two, at in HALVES:
        n = REDUCE_XY
        base = {}
        for u in RING4:
            far, last = {}, {}
            for s, w in SIDES:
                q = 0 if s == 1 else 1
                far[s, q] = p.reduce(two + w, UNIT, [("gt", at(u, 2) + o + UNIT * q)])
            for s, w in SIDES:
                for q in range(0, 2, n // UNIT):
                    pieces = [[("gt", at(u, s) + o + UNIT * e)] + ([("rb", far[s, e])] if (s, e) in far else [])
                              for e in range(q, q + n // UNIT)]
                    row = p.reduce(two + w, n, *pieces)
                    for k in range(n // UNIT):
                        last[s, q + k] = row + UNIT * k
            for q in (0, 1):
                base[u, q] = [("gt", at(u, 0) + o + UNIT * q), ("rb", last[1, q]), ("rb", last[-1, q])]
        far, last = {}, {}
        for s, w in SIDES:
            q = 0 if s == 1 else 1
            far[s, q] = p.reduce(one + w, UNIT, base[2, q])
        for s, w in SIDES:
            for q in range(0, 2, n // UNIT):
                pieces = [base[s, e] + ([("rb", far[s, e])] if (s, e) in far else []) for e in range(q, q + n // UNIT)]
                row = p.reduce(one + w, n, *pieces)
                for k in range(n // UNIT):
                    last[s, q + k] = row + UNIT * k
        for q in (0, 1):
            p.final_txt.append((o + UNIT * q, base[0, q] + [("rb", last[1, q]), ("rb", last[-1, q])]))
    return p


PLAN = make_plan()

ORDER = (
    15, 19, 88, 8, 68, 78, 58, 0, 56, 57, 14, 18, 69, 16, 20, 9, 59, 79, 89, 17, 21, 10, 1, 2, 23, 27, 80, 90, 22,
    26, 83, 93, 53, 54, 60, 71, 24, 28, 63, 73, 25, 29, 55, 52, 81, 91, 11, 70, 3, 61, 4, 31, 35, 30, 34, 49, 50,
    82, 92, 74, 64, 32, 36, 12, 72, 62, 33, 85, 37, 95, 48, 51, 1033, 5, 6, 84, 94, 39, 41, 65, 76, 1023, 86, 96,
    38, 40, 45, 46, 13, 75, 66, 1032, 1022, 87, 97, 47, 44, 7, 67, 77, 1013, 1012, 1220, 43, 42, 1011, 1110, 1031,
    1021, 1210, 1003, 1002, 1030, 1010, 1020, 1200, 1001, 1100, 1000, 1201, 175, 174, 155, 154, 1101, 99, 98, 100,
    167, 166, 147, 101, 150, 1211, 171, 170, 143, 146, 116, 1111, 114, 102, 103, 104, 117, 115, 142, 151, 163, 105,
    162, 1120, 177, 176, 157, 125, 120, 156, 1121, 106, 107, 124, 108, 121, 109, 1221, 168, 169, 122, 149, 118, 152,
    1130, 123, 1131, 119, 173, 110, 172, 153, 148, 112, 133, 128, 111, 113, 1230, 132, 129, 159, 179, 158, 178,
    1231, 130, 126, 165, 145, 164, 144, 131, 127, 141, 136, 140, 137, 161, 160, 181, 180, 138, 134, 139, 135,
)


def unit_rows(v):
    v = v.astype(F32)
    inv = lax.rsqrt(jnp.sum(v * v, axis=1, keepdims=True) + 1e-6)
    return v * inv, inv


def kernel(ie_ref, te_ref, ii_ref, ti_ref, oi_ref, ot_ref,
           ie, te, ids, img, txt, coef, gi, gt, sb, rb, iid, tid, icol, ssem, rsem, isem):
    blk, rep, sub = lax.axis_index("blk"), lax.axis_index("rep"), lax.axis_index("sub")
    where = {
        "x+": {"sub": lax.rem(sub + 1, 4)}, "x-": {"sub": lax.rem(sub + 3, 4)},
        "y+": {"blk": lax.rem(blk + 2, 8)}, "y-": {"blk": lax.rem(blk + 6, 8)},
        "z+": {"rep": lax.rem(rep + 1, 8)}, "z-": {"rep": lax.rem(rep + 7, 8)},
        "c": {"blk": blk + 1 - 2 * lax.rem(blk, 2)},
    }
    barrier = pltpu.get_barrier_semaphore()
    for way in where.values():
        pl.semaphore_signal(barrier, inc=1, device_id=way, device_id_type=MESH)
    loads = [
        pltpu.make_async_copy(src, dst, isem.at[k])
        for k, (src, dst) in enumerate(((ie_ref, ie), (te_ref, te), (ii_ref, ids.at[0]), (ti_ref, ids.at[1])))
    ]
    for load in loads:
        load.start()
    for load in loads:
        load.wait()
    img[pl.ds(img_row(0, 0), ROWS), :] = unit_rows(ie[...])[0].astype(BF16)
    txt[pl.ds(txt_row(0, 0), ROWS), :] = unit_rows(te[...])[0].astype(BF16)
    for k, ref, row in ((0, iid, iid_row(0)), (1, tid, tid_row(0, 0))):
        ref[row] = jnp.concatenate([ids[k], ids[k]], axis=1)
    pl.semaphore_wait(barrier, len(where))

    bufs = {"img": img, "txt": txt, "gi": gi, "gt": gt, "sb": sb, "rb": rb, "iid": iid, "tid": tid}

    def copy(index):
        way, src, dst, _ = PLAN.msgs[index]
        return pltpu.make_async_remote_copy(
            src_ref=bufs[src[0]].at[pl.ds(src[1], src[2])],
            dst_ref=bufs[dst[0]].at[pl.ds(dst[1], dst[2])],
            send_sem=ssem.at[index], recv_sem=rsem.at[index],
            device_id=where[way], device_id_type=MESH,
        )

    here, sent = set(), []

    def need(buf, row, n):
        for r in range(row, row + n):
            name = PLAN.origin.get((buf, r))
            if name is not None and name not in here:
                here.add(name)
                copy(name).wait_recv()

    def total(n, terms):
        acc = None
        for buf, row in terms:
            need(buf, row, n)
            v = bufs[buf][pl.ds(row, n), :].astype(F32)
            acc = v if acc is None else acc + v
        return acc

    def send(name):
        _, src, _, pieces = PLAN.msgs[name]
        if pieces is None:
            need(*src)
        else:
            n = src[2] // len(pieces)
            for k, terms in enumerate(pieces):
                sb[pl.ds(src[1] + n * k, n), :] = total(n, terms).astype(BF16)
        copy(name).start()
        sent.append(name)

    lane = lax.broadcasted_iota(jnp.int32, (1, 128), 1)
    ready = set()

    def columns(row, n):
        for p in range(row // 128, (row + n) // 128):
            if p not in ready:
                ready.add(p)
                need("iid", 2 * p, 2)
                both_ids = jnp.where(lane < 64, iid[2 * p], iid[2 * p + 1])
                icol[pl.ds(128 * p, 128), :] = jnp.transpose(jnp.broadcast_to(both_ids, (128, 128)))

    def tile(i, m, t, n):
        need("img", i, m)
        need("txt", t, n)
        columns(i, m)
        keys = []
        for b in range(t // 64, (t + n) // 64, 2):
            r0, r1 = tid_row(*T_ORDER[b]), tid_row(*T_ORDER[b + 1])
            need("tid", r0, 1)
            need("tid", r1, 1)
            keys.append(jnp.where(lane < 64, tid[r0], tid[r1]))
        z = lax.dot_general(img[pl.ds(i, m), :], txt[pl.ds(t, n), :],
                            (((1,), (1,)), ((), ())), preferred_element_type=F32)
        sig = jax.nn.sigmoid(SCALE * z + BIAS)
        rows = icol[pl.ds(i, m), :]
        same = jnp.concatenate([(rows == k).astype(F32) for k in keys], axis=1)
        coef[pl.ds(i, m), pl.ds(t, n)] = (SCALE * (sig - same)).astype(BF16)

    def gradient(ref, row, n, part, g):
        rows = pl.ds(row, n)
        ref[rows, :] = ref[rows, :] + g if part else g

    for step in ORDER:
        if step < 1000:
            send(step)
            continue
        c, part = step // 10 % 10, step % 10
        if step < 1100:
            tile(*IMG_CHUNKS[c], *TXT_CHUNKS[part])
        elif step < 1200:
            (i, m), first = IMG_CHUNKS[c], TXT_CHUNKS[0][1]
            ks = pl.ds(0, first) if part else pl.ds(first, 1024 - first)
            gradient(gi, i, m, part, jnp.dot(coef[pl.ds(i, m), ks], txt[ks, :], preferred_element_type=F32))
        else:
            (t, n), first = TXT_CHUNKS[c], IMG_CHUNKS[0][1]
            ks = pl.ds(0, first) if part else pl.ds(first, 1024 - first)
            gradient(gt, t, n, part, lax.dot_general(coef[ks, pl.ds(t, n)], img[ks, :], (((0,), (0,)), ((), ())),
                                                     preferred_element_type=F32))
    for pieces, out in ((PLAN.final_img, oi_ref), (PLAN.final_txt, ot_ref)):
        for row, terms in pieces:
            out[pl.ds(row, UNIT), :] = total(UNIT, terms)
    n_msgs = len(PLAN.msgs)
    assert len(sent) == n_msgs and len(here) == n_msgs
    for name in sent:
        copy(name).wait_send()


def project(ie_ref, te_ref, gi_ref, gt_ref, oi_ref, ot_ref):
    for embed, grad, out in ((ie_ref, gi_ref, oi_ref), (te_ref, gt_ref, ot_ref)):
        unit, inv = unit_rows(embed[...])
        g = grad[...]
        along = jnp.sum(unit * g, axis=1, keepdims=True)
        out[...] = (g - unit * along) * inv


def body(image_embed, text_embed, image_ids, text_ids):
    vmem, hbm = pl.BlockSpec(memory_space=pltpu.VMEM), pl.BlockSpec(memory_space=pltpu.HBM)
    n = len(PLAN.msgs)
    out = jax.ShapeDtypeStruct((ROWS, D), F32)
    sums = pl.pallas_call(
        kernel,
        name="pairs",
        out_shape=(out, out),
        in_specs=[hbm] * 4,
        out_specs=(vmem, vmem),
        scratch_shapes=[
            pltpu.VMEM((ROWS, D), BF16),
            pltpu.VMEM((ROWS, D), BF16),
            pltpu.VMEM((2, 1, ROWS), jnp.int32),
            pltpu.VMEM((1024, D), BF16),
            pltpu.VMEM((1024, D), BF16),
            pltpu.VMEM((1024, 1024), BF16),
            pltpu.VMEM((1024, D), F32),
            pltpu.VMEM((1024, D), F32),
            pltpu.VMEM((PLAN.rows["sb"], D), BF16),
            pltpu.VMEM((PLAN.rows["rb"], D), BF16),
            pltpu.VMEM((16, 1, 128), jnp.int32),
            pltpu.VMEM((16, 1, 128), jnp.int32),
            pltpu.VMEM((1024, 128), jnp.int32),
            pltpu.SemaphoreType.DMA((n,)),
            pltpu.SemaphoreType.DMA((n,)),
            pltpu.SemaphoreType.DMA((4,)),
        ],
        compiler_params=pltpu.CompilerParams(
            collective_id=0, has_side_effects=True, vmem_limit_bytes=48 * 1024 * 1024
        ),
    )(*(pltpu.with_memory_space_constraint(a, pltpu.HBM)
        for a in (image_embed, text_embed, image_ids.reshape(1, ROWS), text_ids.reshape(1, ROWS))))
    return pl.pallas_call(
        project,
        name="project",
        out_shape=(out, out),
        in_specs=[vmem] * 4,
        out_specs=(vmem, vmem),
        compiler_params=pltpu.CompilerParams(vmem_limit_bytes=4 * 1024 * 1024),
    )(image_embed, text_embed, *sums)


def solution(mesh):
    rows = P(("blk", "rep", "sub"), None)
    flat = P(("blk", "rep", "sub"))
    return jax.shard_map(
        body, mesh=mesh, in_specs=(rows, rows, flat, flat), out_specs=(rows, rows), check_vma=False
    )
```

time: 58.9 us -> 51.4 us (0.87)
  Pallas kernels: 55.3 us -> 50.4 us
  local copies, waits for them, and re-layouts: 2.46 us -> 0.01 us
    pallas_call x1 -> x2, Pallas kernels: 55.3 us -> 50.4 us  [the longest x1 49.4 us: body(): pl.pallas_call(kernel, name='pairs', out_shape=(out, out), in_specs=[hbm]...]
    unnamed x4, local copies, waits for them, and re-layouts: 2.46 us -> 0.01 us
where the time goes in v2:
time: 51.4 us; the launch traced here: 51.1 us
  Pallas kernels  50.4 us (98%)
  between operations  0.67 us (1%)
    pallas_call x1, Pallas kernels, body(): pl.pallas_call(kernel, name='pairs', out_shape=(out, out), in_specs=[hbm]...  49.4 us
    pallas_call x1, Pallas kernels, body(): pl.pallas_call(project, name='project', out_shape=(out, out), in_specs=[v...  1.03 us

profile of v2, /device:TPU:1, one launch (start us, length us, event | category | flops | bytes accessed | tf_op | source)
XLA Modules:
  0.0 51.1 jit_solution(6252507591322748016)
XLA Ops:
  0.6 0.0 copy-start
  0.6 0.0 copy-start.1
  0.7 49.4 %pairs.1 = (f32[64,1152]{1,0:T(8,128)S(1)}, f32[64,1152]{1,0:T(8,128)S(1)}) custom-call(bf16[64,1152]{1,0:T(8,128)(2,1)} %ie_ref.3, bf16[64,1152]{1,0:T(8,128)(2,1)} %te_ref.3, s32[1,64]{1,0:T(1,128)} %bitcast.2, s32[1,64]{1,0:T(1,128)} %bitcast.3), custom_call_target="tpu_custom_call" | custom-call | tf_op jit(solution)/shard_map/pairs/pallas_call | solution.py:325
  50.0 0.0 copy-done
  50.0 0.0 copy-done.1
  50.0 1.0 %project.1 = (f32[64,1152]{1,0:T(8,128)}, f32[64,1152]{1,0:T(8,128)}) custom-call(bf16[64,1152]{1,0:T(8,128)(2,1)S(1)} %copy-done, bf16[64,1152]{1,0:T(8,128)(2,1)S(1)} %copy-done.1, f32[64,1152]{1,0:T(8,128)S(1)} %get-tuple-element.4.gi_ref, f32[64,1152]{1,0:T(8,128)S(1)} %get-tuple-element.5.gt_ref), custom_call_target="tpu_custom_call" | custom-call | tf_op jit(solution)/shard_map/project/pallas_call | solution.py:354
Async XLA Ops:
  0.6 49.4 %copy-start = (bf16[64,1152]{1,0:T(8,128)(2,1)S(1)}, bf16[64,1152]{1,0:T(8,128)(2,1)}, u32[]{:S(2)}) copy-start(bf16[64,1152]{1,0:T(8,128)(2,1)} %ie_ref.3) | copy-start | bytes 442372
  0.6 49.4 %copy-start.1 = (bf16[64,1152]{1,0:T(8,128)(2,1)S(1)}, bf16[64,1152]{1,0:T(8,128)(2,1)}, u32[]{:S(2)}) copy-start(bf16[64,1152]{1,0:T(8,128)(2,1)} %te_ref.3) | copy-start | bytes 442372

commit v3 on v2

--- a/solution.py
+++ b/solution.py
@@ -14,6 +14,7 @@
 PARTS_Z = {1: ((0, 16), (16, 16), (32, 16), (48, 16)), -1: ((48, 16), (32, 16), (16, 16), (0, 16))}
 IMG_CHUNKS = ((0, 256), (256, 256), (512, 256), (768, 256))
 TXT_CHUNKS = ((0, 256), (256, 256), (512, 256), (768, 256))
+TERMS = ((512, 512), (0, 512))
 MESH = pl.DeviceIdType.MESH
 F32 = jnp.float32
 BF16 = jnp.bfloat16
@@ -168,17 +169,18 @@
 
 
 PLAN = make_plan()
+KIND = {"iid": "iid", "tid": "iid", "img": "img", "txt": "img", "sb": "sb"}
 
 ORDER = (
-    15, 19, 88, 8, 68, 78, 58, 0, 56, 57, 14, 18, 69, 16, 20, 9, 59, 79, 89, 17, 21, 10, 1, 2, 23, 27, 80, 90, 22,
-    26, 83, 93, 53, 54, 60, 71, 24, 28, 63, 73, 25, 29, 55, 52, 81, 91, 11, 70, 3, 61, 4, 31, 35, 30, 34, 49, 50,
-    82, 92, 74, 64, 32, 36, 12, 72, 62, 33, 85, 37, 95, 48, 51, 1033, 5, 6, 84, 94, 39, 41, 65, 76, 1023, 86, 96,
-    38, 40, 45, 46, 13, 75, 66, 1032, 1022, 87, 97, 47, 44, 7, 67, 77, 1013, 1012, 1220, 43, 42, 1011, 1110, 1031,
-    1021, 1210, 1003, 1002, 1030, 1010, 1020, 1200, 1001, 1100, 1000, 1201, 175, 174, 155, 154, 1101, 99, 98, 100,
-    167, 166, 147, 101, 150, 1211, 171, 170, 143, 146, 116, 1111, 114, 102, 103, 104, 117, 115, 142, 151, 163, 105,
-    162, 1120, 177, 176, 157, 125, 120, 156, 1121, 106, 107, 124, 108, 121, 109, 1221, 168, 169, 122, 149, 118, 152,
-    1130, 123, 1131, 119, 173, 110, 172, 153, 148, 112, 133, 128, 111, 113, 1230, 132, 129, 159, 179, 158, 178,
-    1231, 130, 126, 165, 145, 164, 144, 131, 127, 141, 136, 140, 137, 161, 160, 181, 180, 138, 134, 139, 135,
+    78, 58, 88, 68, 15, 18, 0, 57, 56, 16, 19, 59, 8, 69, 9, 79, 89, 14, 20, 1, 21, 17, 2, 23, 26, 83, 63, 93, 73,
+    24, 27, 53, 60, 10, 70, 90, 80, 22, 28, 54, 3, 29, 52, 25, 61, 55, 71, 91, 81, 4, 31, 34, 11, 72, 92, 32, 35,
+    82, 62, 49, 30, 36, 50, 5, 12, 95, 85, 65, 75, 37, 48, 51, 33, 6, 94, 84, 64, 74, 39, 40, 1023, 41, 13, 66, 45,
+    76, 86, 96, 1033, 1230, 38, 46, 77, 97, 87, 67, 1032, 7, 1022, 44, 47, 1120, 1220, 1130, 1012, 1013, 43, 1110,
+    1011, 42, 1021, 1031, 1020, 1030, 1200, 1000, 1010, 1201, 175, 174, 154, 155, 1003, 167, 166, 146, 147, 1001,
+    1002, 1100, 150, 151, 1101, 98, 99, 100, 101, 1111, 105, 104, 102, 103, 114, 117, 177, 176, 156, 115, 116, 1210,
+    1211, 157, 120, 170, 171, 142, 124, 1121, 106, 121, 125, 163, 107, 143, 168, 109, 148, 108, 118, 123, 1221, 169,
+    149, 152, 119, 122, 162, 1231, 128, 132, 173, 172, 179, 178, 129, 133, 153, 1131, 110, 144, 159, 126, 131, 158,
+    111, 113, 112, 165, 127, 145, 130, 164, 136, 140, 137, 141, 180, 181, 134, 139, 160, 161, 135, 138,
 )
 
 
@@ -221,7 +223,7 @@
         return pltpu.make_async_remote_copy(
             src_ref=bufs[src[0]].at[pl.ds(src[1], src[2])],
             dst_ref=bufs[dst[0]].at[pl.ds(dst[1], dst[2])],
-            send_sem=ssem.at[index], recv_sem=rsem.at[index],
+            send_sem=ssem.at[("iid", "img", "sb").index(KIND[src[0]])], recv_sem=rsem.at[index],
             device_id=where[way], device_id_type=MESH,
         )
 
@@ -293,12 +295,10 @@
         if step < 1100:
             tile(*IMG_CHUNKS[c], *TXT_CHUNKS[part])
         elif step < 1200:
-            (i, m), first = IMG_CHUNKS[c], TXT_CHUNKS[0][1]
-            ks = pl.ds(0, first) if part else pl.ds(first, 1024 - first)
+            (i, m), ks = IMG_CHUNKS[c], pl.ds(*TERMS[part])
             gradient(gi, i, m, part, jnp.dot(coef[pl.ds(i, m), ks], txt[ks, :], preferred_element_type=F32))
         else:
-            (t, n), first = TXT_CHUNKS[c], IMG_CHUNKS[0][1]
-            ks = pl.ds(0, first) if part else pl.ds(first, 1024 - first)
+            (t, n), ks = TXT_CHUNKS[c], pl.ds(*TERMS[part])
             gradient(gt, t, n, part, lax.dot_general(coef[ks, pl.ds(t, n)], img[ks, :], (((0,), (0,)), ((), ())),
                                                      preferred_element_type=F32))
     for pieces, out in ((PLAN.final_img, oi_ref), (PLAN.final_txt, ot_ref)):
@@ -306,8 +306,10 @@
             out[pl.ds(row, UNIT), :] = total(UNIT, terms)
     n_msgs = len(PLAN.msgs)
     assert len(sent) == n_msgs and len(here) == n_msgs
-    for name in sent:
-        copy(name).wait_send()
+    for kind, ref in (("iid", tid), ("img", sb), ("sb", sb)):
+        n = sum(src[2] for _, src, _, _ in PLAN.msgs if KIND[src[0]] == kind)
+        k = ("iid", "img", "sb").index(kind)
+        pltpu.make_async_copy(ref.at[pl.ds(0, n)], ref.at[pl.ds(0, n)], ssem.at[k]).wait()
 
 
 def project(ie_ref, te_ref, gi_ref, gt_ref, oi_ref, ot_ref):
@@ -340,9 +342,9 @@
             pltpu.VMEM((PLAN.rows["sb"], D), BF16),
             pltpu.VMEM((PLAN.rows["rb"], D), BF16),
             pltpu.VMEM((16, 1, 128), jnp.int32),
-            pltpu.VMEM((16, 1, 128), jnp.int32),
+            pltpu.VMEM((32, 1, 128), jnp.int32),
             pltpu.VMEM((1024, 128), jnp.int32),
-            pltpu.SemaphoreType.DMA((n,)),
+            pltpu.SemaphoreType.DMA((3,)),
             pltpu.SemaphoreType.DMA((n,)),
             pltpu.SemaphoreType.DMA((4,)),
         ],

time: 51.4 us -> 49.1 us (0.955)
  Pallas kernels: 50.4 us -> 48.3 us
    pallas_call x1, Pallas kernels: 49.4 us -> 47.3 us  [body(): pl.pallas_call(kernel, name='pairs', out_shape=(out, out), in_specs=[hbm]...]
where the time goes in v3:
time: 49.1 us; the launch traced here: 49 us
  Pallas kernels  48.3 us (98%)
  between operations  0.67 us (1%)
    pallas_call x1, Pallas kernels, body(): pl.pallas_call(kernel, name='pairs', out_shape=(out, out), in_specs=[hbm]...  47.3 us
    pallas_call x1, Pallas kernels, body(): pl.pallas_call(project, name='project', out_shape=(out, out), in_specs=[v...  1.03 us

profile of v3, /device:TPU:1, one launch (start us, length us, event | category | flops | bytes accessed | tf_op | source)
XLA Modules:
  0.0 49.0 jit_solution(13017588324114661380)
XLA Ops:
  0.6 0.0 copy-start
  0.6 0.0 copy-start.1
  0.7 47.3 %pairs.1 = (f32[64,1152]{1,0:T(8,128)S(1)}, f32[64,1152]{1,0:T(8,128)S(1)}) custom-call(bf16[64,1152]{1,0:T(8,128)(2,1)} %ie_ref.3, bf16[64,1152]{1,0:T(8,128)(2,1)} %te_ref.3, s32[1,64]{1,0:T(1,128)} %bitcast.2, s32[1,64]{1,0:T(1,128)} %bitcast.3), custom_call_target="tpu_custom_call" | custom-call | tf_op jit(solution)/shard_map/pairs/pallas_call | solution.py:327
  48.0 0.0 copy-done
  48.0 0.0 copy-done.1
  48.0 1.0 %project.1 = (f32[64,1152]{1,0:T(8,128)}, f32[64,1152]{1,0:T(8,128)}) custom-call(bf16[64,1152]{1,0:T(8,128)(2,1)S(1)} %copy-done, bf16[64,1152]{1,0:T(8,128)(2,1)S(1)} %copy-done.1, f32[64,1152]{1,0:T(8,128)S(1)} %get-tuple-element.4.gi_ref, f32[64,1152]{1,0:T(8,128)S(1)} %get-tuple-element.5.gt_ref), custom_call_target="tpu_custom_call" | custom-call | tf_op jit(solution)/shard_map/project/pallas_call | solution.py:356
Async XLA Ops:
  0.6 47.4 %copy-start = (bf16[64,1152]{1,0:T(8,128)(2,1)S(1)}, bf16[64,1152]{1,0:T(8,128)(2,1)}, u32[]{:S(2)}) copy-start(bf16[64,1152]{1,0:T(8,128)(2,1)} %ie_ref.3) | copy-start | bytes 442372
  0.6 47.4 %copy-start.1 = (bf16[64,1152]{1,0:T(8,128)(2,1)S(1)}, bf16[64,1152]{1,0:T(8,128)(2,1)}, u32[]{:S(2)}) copy-start(bf16[64,1152]{1,0:T(8,128)(2,1)} %te_ref.3) | copy-start | bytes 442372

commit v4 on v3

--- a/solution.py
+++ b/solution.py
@@ -184,6 +184,44 @@
 )
 
 
+def wanted(step):
+    if step < 1000:
+        _, src, _, pieces = PLAN.msgs[step]
+        if pieces is None:
+            return [src]
+        n = src[2] // len(pieces)
+        return [(buf, row, n) for terms in pieces for buf, row in terms]
+    if step < 1100:
+        (i, m), (t, n) = IMG_CHUNKS[step // 10 % 10], TXT_CHUNKS[step % 10]
+        return [("img", i, m), ("txt", t, n)]
+    return []
+
+
+def group_waits():
+    group, rows = {}, []
+    steps = [wanted(step) for step in ORDER]
+    steps += [[(buf, row, UNIT) for _, terms in final for buf, row in terms] for final in (PLAN.final_img, PLAN.final_txt)]
+    for regions in steps:
+        new = []
+        for buf, row, n in regions:
+            for r in range(row, row + n):
+                index = PLAN.origin.get((buf, r))
+                if index is not None and buf not in ("iid", "tid") and index not in group and index not in new:
+                    new.append(index)
+        for index in new:
+            group[index] = len(rows)
+        if new:
+            rows.append(sum(PLAN.msgs[index][2][2] for index in new))
+    for index in range(len(PLAN.msgs)):
+        if index not in group:
+            group[index] = len(rows)
+            rows.append(0)
+    return group, rows
+
+
+GROUP, GROUP_ROWS = group_waits()
+
+
 def unit_rows(v):
     v = v.astype(F32)
     inv = lax.rsqrt(jnp.sum(v * v, axis=1, keepdims=True) + 1e-6)
@@ -223,7 +261,7 @@
         return pltpu.make_async_remote_copy(
             src_ref=bufs[src[0]].at[pl.ds(src[1], src[2])],
             dst_ref=bufs[dst[0]].at[pl.ds(dst[1], dst[2])],
-            send_sem=ssem.at[("iid", "img", "sb").index(KIND[src[0]])], recv_sem=rsem.at[index],
+            send_sem=ssem.at[("iid", "img", "sb").index(KIND[src[0]])], recv_sem=rsem.at[GROUP[index]],
             device_id=where[way], device_id_type=MESH,
         )
 
@@ -233,8 +271,13 @@
         for r in range(row, row + n):
             name = PLAN.origin.get((buf, r))
             if name is not None and name not in here:
-                here.add(name)
-                copy(name).wait_recv()
+                g = GROUP[name]
+                here.update(k for k in GROUP if GROUP[k] == g)
+                if GROUP_ROWS[g]:
+                    whole = rb.at[pl.ds(0, GROUP_ROWS[g])]
+                    pltpu.make_async_copy(whole, whole, rsem.at[g]).wait()
+                else:
+                    copy(name).wait_recv()
 
     def total(n, terms):
         acc = None
@@ -322,7 +365,6 @@
 
 def body(image_embed, text_embed, image_ids, text_ids):
     vmem, hbm = pl.BlockSpec(memory_space=pltpu.VMEM), pl.BlockSpec(memory_space=pltpu.HBM)
-    n = len(PLAN.msgs)
     out = jax.ShapeDtypeStruct((ROWS, D), F32)
     sums = pl.pallas_call(
         kernel,
@@ -345,7 +387,7 @@
             pltpu.VMEM((32, 1, 128), jnp.int32),
             pltpu.VMEM((1024, 128), jnp.int32),
             pltpu.SemaphoreType.DMA((3,)),
-            pltpu.SemaphoreType.DMA((n,)),
+            pltpu.SemaphoreType.DMA((len(GROUP_ROWS),)),
             pltpu.SemaphoreType.DMA((4,)),
         ],
         compiler_params=pltpu.CompilerParams(

time: 49.1 us -> 48.4 us (0.986)
  Pallas kernels: 48.3 us -> 47.7 us
    pallas_call x1, Pallas kernels: 47.3 us -> 46.6 us  [body(): pl.pallas_call(kernel, name='pairs', out_shape=(out, out), in_specs=[hbm]...]
where the time goes in v4:
time: 48.4 us; the launch traced here: 48.3 us
  Pallas kernels  47.7 us (99%)
  between operations  0.67 us (1%)
    pallas_call x1, Pallas kernels, body(): pl.pallas_call(kernel, name='pairs', out_shape=(out, out), in_specs=[hbm]...  46.6 us
    pallas_call x1, Pallas kernels, body(): pl.pallas_call(project, name='project', out_shape=(out, out), in_specs=[v...  1.03 us

profile of v4, /device:TPU:1, one launch (start us, length us, event | category | flops | bytes accessed | tf_op | source)
XLA Modules:
  0.0 48.3 jit_solution(14292443951965918014)
XLA Ops:
  0.6 0.0 copy-start
  0.6 0.0 copy-start.1
  0.7 46.6 %pairs.1 = (f32[64,1152]{1,0:T(8,128)S(1)}, f32[64,1152]{1,0:T(8,128)S(1)}) custom-call(bf16[64,1152]{1,0:T(8,128)(2,1)} %ie_ref.3, bf16[64,1152]{1,0:T(8,128)(2,1)} %te_ref.3, s32[1,64]{1,0:T(1,128)} %bitcast.2, s32[1,64]{1,0:T(1,128)} %bitcast.3), custom_call_target="tpu_custom_call" | custom-call | tf_op jit(solution)/shard_map/pairs/pallas_call | solution.py:369
  47.3 0.0 copy-done
  47.3 0.0 copy-done.1
  47.3 1.0 %project.1 = (f32[64,1152]{1,0:T(8,128)}, f32[64,1152]{1,0:T(8,128)}) custom-call(bf16[64,1152]{1,0:T(8,128)(2,1)S(1)} %copy-done, bf16[64,1152]{1,0:T(8,128)(2,1)S(1)} %copy-done.1, f32[64,1152]{1,0:T(8,128)S(1)} %get-tuple-element.4.gi_ref, f32[64,1152]{1,0:T(8,128)S(1)} %get-tuple-element.5.gt_ref), custom_call_target="tpu_custom_call" | custom-call | tf_op jit(solution)/shard_map/project/pallas_call | solution.py:398
Async XLA Ops:
  0.6 46.7 %copy-start = (bf16[64,1152]{1,0:T(8,128)(2,1)S(1)}, bf16[64,1152]{1,0:T(8,128)(2,1)}, u32[]{:S(2)}) copy-start(bf16[64,1152]{1,0:T(8,128)(2,1)} %ie_ref.3) | copy-start | bytes 442372
  0.6 46.7 %copy-start.1 = (bf16[64,1152]{1,0:T(8,128)(2,1)S(1)}, bf16[64,1152]{1,0:T(8,128)(2,1)}, u32[]{:S(2)}) copy-start(bf16[64,1152]{1,0:T(8,128)(2,1)} %te_ref.3) | copy-start | bytes 442372

commit v5 on v4

--- a/solution.py
+++ b/solution.py
@@ -355,12 +355,17 @@
         pltpu.make_async_copy(ref.at[pl.ds(0, n)], ref.at[pl.ds(0, n)], ssem.at[k]).wait()
 
 
-def project(ie_ref, te_ref, gi_ref, gt_ref, oi_ref, ot_ref):
-    for embed, grad, out in ((ie_ref, gi_ref, oi_ref), (te_ref, gt_ref, ot_ref)):
+def project(ie_ref, te_ref, gi_ref, gt_ref, oi_ref, ot_ref, made, sem):
+    writes = []
+    for k, (embed, grad, out) in enumerate(((ie_ref, gi_ref, oi_ref), (te_ref, gt_ref, ot_ref))):
         unit, inv = unit_rows(embed[...])
         g = grad[...]
         along = jnp.sum(unit * g, axis=1, keepdims=True)
-        out[...] = (g - unit * along) * inv
+        made[k] = (g - unit * along) * inv
+        writes.append(pltpu.make_async_copy(made.at[k], out, sem.at[k]))
+        writes[k].start()
+    for write in writes:
+        write.wait()
 
 
 def body(image_embed, text_embed, image_ids, text_ids):
@@ -400,7 +405,8 @@
         name="project",
         out_shape=(out, out),
         in_specs=[vmem] * 4,
-        out_specs=(vmem, vmem),
+        out_specs=(hbm, hbm),
+        scratch_shapes=[pltpu.VMEM((2, ROWS, D), F32), pltpu.SemaphoreType.DMA((2,))],
         compiler_params=pltpu.CompilerParams(vmem_limit_bytes=4 * 1024 * 1024),
     )(image_embed, text_embed, *sums)
 

time: 48.4 us -> 48.4 us (level)
  no operation moved by 1% of the time
where the time goes in v5:
time: 48.4 us; the launch traced here: 48.3 us
  Pallas kernels  47.7 us (99%)
  between operations  0.67 us (1%)
    pallas_call x1, Pallas kernels, body(): pl.pallas_call(kernel, name='pairs', out_shape=(out, out), in_specs=[hbm]...  46.6 us
    pallas_call x1, Pallas kernels, body(): pl.pallas_call(project, name='project', out_shape=(out, out), in_specs=[v...  1.04 us

profile of v5, /device:TPU:1, one launch (start us, length us, event | category | flops | bytes accessed | tf_op | source)
XLA Modules:
  0.0 48.3 jit_solution(16977886431083662363)
XLA Ops:
  0.6 0.0 copy-start
  0.6 0.0 copy-start.1
  0.7 46.6 %pairs.1 = (f32[64,1152]{1,0:T(8,128)S(1)}, f32[64,1152]{1,0:T(8,128)S(1)}) custom-call(bf16[64,1152]{1,0:T(8,128)(2,1)} %ie_ref.3, bf16[64,1152]{1,0:T(8,128)(2,1)} %te_ref.3, s32[1,64]{1,0:T(1,128)} %bitcast.2, s32[1,64]{1,0:T(1,128)} %bitcast.3), custom_call_target="tpu_custom_call" | custom-call | tf_op jit(solution)/shard_map/pairs/pallas_call | solution.py:374
  47.3 0.0 copy-done
  47.3 0.0 copy-done.1
  47.3 1.0 %project.1 = (f32[64,1152]{1,0:T(8,128)}, f32[64,1152]{1,0:T(8,128)}) custom-call(bf16[64,1152]{1,0:T(8,128)(2,1)S(1)} %copy-done, bf16[64,1152]{1,0:T(8,128)(2,1)S(1)} %copy-done.1, f32[64,1152]{1,0:T(8,128)S(1)} %get-tuple-element.4.gi_ref, f32[64,1152]{1,0:T(8,128)S(1)} %get-tuple-element.5.gt_ref), custom_call_target="tpu_custom_call" | custom-call | tf_op jit(solution)/shard_map/project/pallas_call | solution.py:403
Async XLA Ops:
  0.6 46.7 %copy-start = (bf16[64,1152]{1,0:T(8,128)(2,1)S(1)}, bf16[64,1152]{1,0:T(8,128)(2,1)}, u32[]{:S(2)}) copy-start(bf16[64,1152]{1,0:T(8,128)(2,1)} %ie_ref.3) | copy-start | bytes 442372
  0.6 46.7 %copy-start.1 = (bf16[64,1152]{1,0:T(8,128)(2,1)S(1)}, bf16[64,1152]{1,0:T(8,128)(2,1)}, u32[]{:S(2)}) copy-start(bf16[64,1152]{1,0:T(8,128)(2,1)} %te_ref.3) | copy-start | bytes 442372
